TPU v7x, 32 devices: a whole 2x2x4 slice. The times are simulated.
32 devices in a mesh: chan: 8 (over y, x, core), tm: 4 (over z).
Axes of the slice: x: 2, y: 2, z: 4, core: 2. Of those that a mesh axis runs over, the one named last changes fastest.
Arguments:
- voltages: bfloat16 [2, 8, 2048, 512], P(None, None, 'chan', 'tm'), may hold values from -0.25 to 0.25
- assignment: int32 [1024, 1], replicated, may hold values from 0 to 7; in each aligned block of 1024 rows (0 to 1023, 1024 to 2047, ...) at most 192 rows name the same one
- slot_subarray_index: int32 [8], replicated, may hold values from 0 to 7, each once
Outputs:
- visibilities: float32 [8, 8, 2, 384, 384], P('tm', 'chan')
Inputs may be any that keep to these rules, and one draw needn't show every extreme that they name: `assignment`: no subarray holds more than 192 antennas; one holds exactly 192. `slot_subarray_index`: each subarray appears once.
All inputs are finite; a program needn't handle non-finite values.
Results may differ from a plain program's by a relative error of at most 0.008.
Values may be sent and summed in bfloat16 or wider, within the bound.
No kernel may reach another device: no remote copies, remote signals or barrier semaphores. Data moves between devices by JAX's collectives and lax.ppermute only.
A program may use at most 64 MiB of HBM per device.

v0:
```python
import jax
import jax.numpy as jnp
from jax import lax
from jax.sharding import PartitionSpec as P

SLOT = 384


def result_slot_lookup(assignment, slot_subarray_index, subarrays, slots, inputs):
    owner = jnp.repeat(assignment[:, 0], 2)
    onehot = (owner[:, None] == jnp.arange(subarrays, dtype=jnp.int32)[None, :]).astype(jnp.int32)
    ranks = jnp.sum((jnp.cumsum(onehot, axis=0) - onehot) * onehot, axis=1)
    table = jnp.full((subarrays, slots), inputs, jnp.int32)
    table = table.at[owner, ranks].set(jnp.arange(inputs, dtype=jnp.int32))
    return table[slot_subarray_index].reshape(-1)


def compact(block, rows, subarrays, slots):
    parts, chans, inputs, samples = block.shape
    padded_voltages = jnp.concatenate(
        [block, jnp.zeros((parts, chans, 1, samples), block.dtype)], axis=2
    )
    picked = jnp.take(padded_voltages, rows, axis=2)
    picked = picked.reshape(parts, chans, subarrays, slots, samples)
    picked = jnp.transpose(picked, (2, 1, 0, 3, 4))
    return picked.reshape(subarrays, chans, 2 * slots, samples)


def gram(stacked):
    full = jnp.einsum("...pt,...qt->...pq", stacked, stacked, preferred_element_type=jnp.float32)
    half = stacked.shape[-2] // 2
    real = full[..., :half, :half] + full[..., half:, half:]
    imag = full[..., half:, :half] - full[..., :half, half:]
    return jnp.stack([real, imag], axis=-3)


def shards(voltages, assignment, slot_subarray_index):
    subarrays = slot_subarray_index.shape[0]
    slots = SLOT
    inputs = 2 * assignment.shape[0]
    rows = result_slot_lookup(assignment, slot_subarray_index, subarrays, slots, inputs)
    local_samples = voltages.shape[3]
    time_groups = lax.axis_size("tm")
    stacked = compact(
        lax.all_to_all(voltages, "chan", split_axis=1, concat_axis=2, tiled=True),
        rows,
        subarrays,
        slots,
    )
    received = lax.all_to_all(stacked, "tm", split_axis=0, concat_axis=3, tiled=True)
    total = None
    for block_index in range(time_groups):
        piece = received[..., block_index * local_samples : (block_index + 1) * local_samples]
        rounded = gram(piece).astype(jnp.bfloat16).astype(jnp.float32)
        total = rounded if total is None else total + rounded
    return total


def solution(mesh):
    placed = (P(None, None, "chan", "tm"), P(), P())
    return jax.shard_map(
        shards,
        mesh=mesh,
        in_specs=placed,
        out_specs=P("tm", "chan", None, None, None),
        check_vma=False,
    )
```

profile of v0, /device:TPU:0, one launch (start us, length us, event | category | flops | bytes accessed | tf_op | source)
XLA Modules:
  0.0 84.1 jit_solution(1011175587574448796)
XLA Ops:
  0.0 2.3 %copy.13 = bf16[2,8,256,128]{3,2,0,1:T(8,128)(2,1)} copy(bf16[2,8,256,128]{3,2,1,0:T(8,128)(2,1)} %param.3) | data formatting | bytes 2097152 | tf_op args[0]
  2.3 0.0 copy-start
  2.3 0.0 copy-start.3
  2.3 5.3 %all-to-all-start = ((bf16[2,8,256,128]{3,2,0,1:T(8,128)(2,1)}), bf16[2,8,256,128]{3,2,0,1:T(8,128)(2,1)S(1)}, u32[]{:S(2)}, u32[]{:S(2)}) async-start(bf16[2,8,256,128]{3,2,0,1:T(8,128)(2,1)} %copy.13), calls=%async_computation | async-start | bytes 2097152 | tf_op jit(solution)/shard_map/all_to_all | solution.py:45
  7.6 0.0 copy-start.2
  7.6 0.0 copy-start.1
  7.6 0.0 copy-done
  7.7 0.2 broadcast_in_dim.30
  7.9 0.3 eq.23
  8.1 0.3 reshape.321
  8.4 0.0 copy-done.3
  8.5 0.6 broadcast.137
  9.1 0.7 reduce.9
  9.8 0.1 broadcast_in_dim.31
  9.9 0.1 copy.11
  10.0 0.1 copy.12
  10.0 2.3 %reduce-window.6 = s32[8,16,128]{2,1,0:T(8,128)S(1)} reduce-window(s32[8,16,128]{2,1,0:T(8,128)S(1)} %fusion.19, s32[]{:T(128)} %constant.11.clone.1), window={size=1x1x128 pad=0_0x0_0x127_0}, to_apply=%region_0.0 | reduce-window | flops 2080768 | bytes 131076 | tf_op jit(solution)/shard_map/reduce-window
  12.3 0.3 slice_reduce_fusion
  12.6 0.2 reduce-window.9
  12.8 0.1 add_bitcast_fusion
  13.0 0.0 copy-done.2
  13.0 0.1 and_reduce_fusion
  13.1 0.0 copy-done.1
  13.1 0.1 multiply_reduce_fusion
  13.2 8.1 %scatter_custom_fusion = s32[3072]{0:T(1024)S(1)} fusion(s32[2048]{0:T(1024)S(1)} %broadcast_select_fusion, s32[2048]{0:T(1024)S(1)} %iota.11, s32[]{:T(128)} %constant.10.clone.1), kind=kCustom, calls=%fused_computation.57 | custom fusion | bytes 12292
  21.3 0.6 gather_fusion
  21.9 1.1 %all-to-all-done = bf16[2,8,256,128]{3,2,0,1:T(8,128)(2,1)S(1)} async-done(((bf16[2,8,256,128]{3,2,0,1:T(8,128)(2,1)}), bf16[2,8,256,128]{3,2,0,1:T(8,128)(2,1)S(1)}, u32[]{:S(2)}, u32[]{:S(2)}) %all-to-all-start) | async-done | bytes 1048608 | tf_op jit(solution)/shard_map/all_to_all | solution.py:45
  23.0 1.1 %copy.14 = bf16[2,8,256,128]{3,0,2,1:T(2,128)(2,1)S(1)} copy(bf16[2,8,256,128]{3,2,0,1:T(8,128)(2,1)S(1)} %all-to-all-done) | data formatting | bytes 2097152 | tf_op jit(solution)/shard_map/all_to_all | solution.py:45
  24.1 1.0 %pad_bitcast_fusion = bf16[2,2049,128]{2,0,1:T(2,128)(2,1)S(1)} fusion(bf16[2,1,2048,128]{3,0,2,1:T(2,128)(2,1)S(1)} %bitcast.90), kind=kLoop, calls=%fused_computation.26 | loop fusion | bytes 2097664 | tf_op jit(solution)/shard_map/concatenate | solution.py:20
  25.1 10.4 %gather_fusion.1 = bf16[3072,2,128]{2,1,0:T(2,128)(2,1)S(1)} fusion(bf16[2,2049,128]{2,0,1:T(2,128)(2,1)S(1)} %pad_bitcast_fusion, s32[3072]{0:T(1024)S(1)} %broadcast_clamp_fusion), kind=kCustom, calls=%fused_computation.1 | custom fusion | bytes 3158016 | tf_op jit(solution)/shard_map/jit(_take)/gather | solution.py:23
  35.5 0.8 copy_select_fusion
  36.3 41.2 %all_to_all.30 = bf16[8,1,768,128]{3,2,1,0:T(8,128)(2,1)S(1)} all-to-all(bf16[8,1,768,128]{3,2,1,0:T(8,128)(2,1)S(1)} %bitcast.88), channel_id=1, replica_groups=mesh['chan'=8,'tm'=4] {'tm'}, dimensions={0} | all-to-all | bytes 3145728 | tf_op jit(solution)/shard_map/all_to_all | solution.py:50
  77.5 0.3 copy.25
  77.8 0.8 convolution_bitcast_fusion
  78.6 0.8 convolution_bitcast_fusion.1
  79.3 0.8 convolution_bitcast_fusion.2
  80.1 0.8 convolution_bitcast_fusion.3
  80.9 0.3 fusion.14
  81.2 0.3 fusion.12
  81.4 0.3 fusion.10
  81.7 0.3 fusion.8
  82.0 0.5 convert_add_fusion
  82.5 1.6 %copy.18 = f32[2,1,2,384,384]{4,3,2,1,0:T(8,128)} copy(f32[2,1,2,384,384]{4,3,0,2,1:T(8,128)S(1)} %convert_add_fusion) | data formatting | bytes 4718592 | tf_op jit(solution)/shard_map/add | solution.py:55
  (13 shorter events, 0.2 us)
Async XLA Ops:
  2.3 5.4 %copy-start = (s32[1024,1]{0,1:T(1,128)S(1)}, s32[1024,1]{0,1:T(1,128)}, u32[]{:S(2)}) copy-start(s32[1024,1]{0,1:T(1,128)} %param.4) | copy-start | bytes 12292
  2.3 6.1 %copy-start.3 = (s32[8]{0:T(128)S(1)}, s32[8]{0:T(128)}, u32[]{:S(2)}) copy-start(s32[8]{0:T(128)} %param.5) | copy-start | bytes 100
  2.3 20.7 %all-to-all-start = ((bf16[2,8,256,128]{3,2,0,1:T(8,128)(2,1)}), bf16[2,8,256,128]{3,2,0,1:T(8,128)(2,1)S(1)}, u32[]{:S(2)}, u32[]{:S(2)}) async-start(bf16[2,8,256,128]{3,2,0,1:T(8,128)(2,1)} %copy.13), calls=%async_computation | async-start | bytes 2097152 | tf_op jit(solution)/shard_map/all_to_all | solution.py:45
  7.6 5.3 %copy-start.2 = (s32[2]{0:T(128)S(1)}, s32[2]{0:T(128)}, u32[]{:S(2)}) copy-start(s32[2]{0:T(128)} %constant.36) | copy-start | bytes 28
  7.6 5.4 %copy-start.1 = (s32[2]{0:T(128)S(1)}, s32[2]{0:T(128)}, u32[]{:S(2)}) copy-start(s32[2]{0:T(128)} %constant.33) | copy-start | bytes 28
where the time goes:
time: 84.3 us; the launch traced here: 84.1 us
  blocking collectives  41.2 us (49%)
  local copies, waits for them, and re-layouts  27.2 us (32%)
  other arithmetic  5.91 us (7%)
  starting transfers between devices  5.33 us (6%)
  matrix products  3.09 us (4%)
  waiting for transfers between devices  1.08 us (1%)
    all_to_all x1, blocking collectives, shards(): lax.all_to_all(stacked, 'tm', split_axis=0, concat_axis=3, tiled=True)  41.2 us
    unnamed x12, local copies, waits for them, and re-layouts  11 us
    gather x1, local copies, waits for them, and re-layouts, compact(): picked = jnp.take(padded_voltages, rows, axis=2)  10.4 us
    all_to_all x1, starting transfers between devices, shards(): lax.all_to_all(voltages, 'chan', split_axis=1, concat_axis=2, tiled=True)  5.33 us
    dot_general x4, matrix products, gram(): jnp.einsum('...pt,...qt->...pq', stacked, stacked, preferred_element_type...  3.09 us
    another operation x2, other arithmetic  2.45 us
  transfers between devices with their start and end apart: 1, of which 1 were waited for; matrix products, arithmetic and copies ran while one was open for 17% of the time, Pallas kernels for 0%

commit v1 on v0

--- a/solution.py
+++ b/solution.py
@@ -42,7 +42,12 @@
     local_samples = voltages.shape[3]
     time_groups = lax.axis_size("tm")
     stacked = compact(
-        lax.all_to_all(voltages, "chan", split_axis=1, concat_axis=2, tiled=True),
+        jnp.concatenate(
+            lax.all_to_all(
+                jnp.stack(jnp.split(voltages, lax.axis_size("chan"), axis=1)), "chan", 0, 0
+            ),
+            axis=2,
+        ),
         rows,
         subarrays,
         slots,

time: 84.3 us -> 102 us (1.21)
  local copies, waits for them, and re-layouts: 27.2 us -> 45.1 us
    unnamed x12 -> x18, local copies, waits for them, and re-layouts: 11 us -> 19.7 us
    reshape x0 -> x1, local copies, waits for them, and re-layouts: none -> 8.68 us  [shards(): jnp.concatenate(lax.all_to_all(jnp.stack(jnp.split(voltages, lax.axis_siz...]
    another operation x0 -> x1, local copies, waits for them, and re-layouts: none -> 1.57 us  [shards(): jnp.stack(jnp.split(voltages, lax.axis_size('chan'), axis=1))]
  transfers between devices with their start and end apart: 1 -> 1, of which waited for: 1 -> 1; matrix products, arithmetic and copies ran while one was open for 17% -> 14% of each run, Pallas kernels for 0% -> 0%
where the time goes in v1:
time: 102 us
  local copies, waits for them, and re-layouts  45.1 us (44%)
  blocking collectives  41.2 us (40%)
  other arithmetic  5.91 us (6%)
  starting transfers between devices  5.33 us (5%)
  matrix products  3.09 us (3%)
  waiting for transfers between devices  1.08 us (1%)
    all_to_all x1, blocking collectives, shards(): lax.all_to_all(stacked, 'tm', split_axis=0, concat_axis=3, tiled=True)  41.2 us
    unnamed x18, local copies, waits for them, and re-layouts  19.7 us
    gather x1, local copies, waits for them, and re-layouts, compact(): picked = jnp.take(padded_voltages, rows, axis=2)  10.4 us
    reshape x1, local copies, waits for them, and re-layouts, shards(): jnp.concatenate(lax.all_to_all(jnp.stack(jnp.split(voltages, lax.axis_siz...  8.68 us
    all_to_all x1, starting transfers between devices, shards(): lax.all_to_all(jnp.stack(jnp.split(voltages, lax.axis_size('chan'), axis=...  5.33 us
    dot_general x4, matrix products, gram(): jnp.einsum('...pt,...qt->...pq', stacked, stacked, preferred_element_type...  3.09 us
    another operation x2, other arithmetic  2.45 us
  transfers between devices with their start and end apart: 1, of which 1 were waited for; matrix products, arithmetic and copies ran while one was open for 14% of the time, Pallas kernels for 0%

profile of v1, /device:TPU:0, one launch (start us, length us, event | category | flops | bytes accessed | tf_op | source)
XLA Modules:
  0.0 102.0 jit_solution(3672793290934902290)
XLA Ops:
  0.0 1.6 %bitcast_dynamic-update-slice_fusion.7 = bf16[8,2,1,256,128]{4,3,1,2,0:T(8,128)(2,1)} fusion(bf16[2,8,256,128]{3,2,1,0:T(8,128)(2,1)} %param.3), kind=kLoop, calls=%fused_computation.46 | loop fusion | bytes 262144
  1.6 1.6 %bitcast_dynamic-update-slice_fusion.6 = bf16[8,2,1,256,128]{4,3,1,2,0:T(8,128)(2,1)} fusion(bf16[8,2,1,256,128]{4,3,1,2,0:T(8,128)(2,1)} %bitcast_dynamic-update-slice_fusion.7, bf16[2,8,256,128]{3,2,1,0:T(8,128)(2,1)} %param.3), kind=kLoop, calls=%fused_computation.45 | loop fusion | bytes 262144
  3.1 1.6 %bitcast_dynamic-update-slice_fusion.5 = bf16[8,2,1,256,128]{4,3,1,2,0:T(8,128)(2,1)} fusion(bf16[8,2,1,256,128]{4,3,1,2,0:T(8,128)(2,1)} %bitcast_dynamic-update-slice_fusion.6, bf16[2,8,256,128]{3,2,1,0:T(8,128)(2,1)} %param.3), kind=kLoop, calls=%fused_computation.44 | loop fusion | bytes 262144
  4.7 1.6 %bitcast_dynamic-update-slice_fusion.4 = bf16[8,2,1,256,128]{4,3,1,2,0:T(8,128)(2,1)} fusion(bf16[8,2,1,256,128]{4,3,1,2,0:T(8,128)(2,1)} %bitcast_dynamic-update-slice_fusion.5, bf16[2,8,256,128]{3,2,1,0:T(8,128)(2,1)} %param.3), kind=kLoop, calls=%fused_computation.43 | loop fusion | bytes 262144
  6.3 1.6 %bitcast_dynamic-update-slice_fusion.3 = bf16[8,2,1,256,128]{4,3,1,2,0:T(8,128)(2,1)} fusion(bf16[8,2,1,256,128]{4,3,1,2,0:T(8,128)(2,1)} %bitcast_dynamic-update-slice_fusion.4, bf16[2,8,256,128]{3,2,1,0:T(8,128)(2,1)} %param.3), kind=kLoop, calls=%fused_computation.42 | loop fusion | bytes 262144
  7.9 1.6 %bitcast_dynamic-update-slice_fusion.2 = bf16[8,2,1,256,128]{4,3,1,2,0:T(8,128)(2,1)} fusion(bf16[8,2,1,256,128]{4,3,1,2,0:T(8,128)(2,1)} %bitcast_dynamic-update-slice_fusion.3, bf16[2,8,256,128]{3,2,1,0:T(8,128)(2,1)} %param.3), kind=kLoop, calls=%fused_computation.41 | loop fusion | bytes 262144
  9.4 1.6 %bitcast_dynamic-update-slice_fusion.1 = bf16[8,2,1,256,128]{4,3,1,2,0:T(8,128)(2,1)} fusion(bf16[8,2,1,256,128]{4,3,1,2,0:T(8,128)(2,1)} %bitcast_dynamic-update-slice_fusion.2, bf16[2,8,256,128]{3,2,1,0:T(8,128)(2,1)} %param.3), kind=kLoop, calls=%fused_computation.40 | loop fusion | bytes 262144
  11.0 1.6 %bitcast_dynamic-update-slice_fusion = bf16[8,2,1,256,128]{4,3,1,2,0:T(8,128)(2,1)} fusion(bf16[8,2,1,256,128]{4,3,1,2,0:T(8,128)(2,1)} %bitcast_dynamic-update-slice_fusion.1, bf16[2,8,256,128]{3,2,1,0:T(8,128)(2,1)} %param.3), kind=kLoop, calls=%fused_computation.39 | loop fusion | bytes 262144 | tf_op jit(solution)/shard_map/stack | solution.py:47
  12.6 5.3 %all-to-all-start = ((bf16[8,2,1,256,128]{4,3,1,2,0:T(8,128)(2,1)}), bf16[8,2,1,256,128]{4,3,1,2,0:T(8,128)(2,1)S(1)}, u32[]{:S(2)}, u32[]{:S(2)}) async-start(bf16[8,2,1,256,128]{4,3,1,2,0:T(8,128)(2,1)} %bitcast_dynamic-update-slice_fusion), calls=%async_computation | async-start | bytes 2097152 | tf_op jit(solution)/shard_map/all_to_all | solution.py:46
  17.9 0.0 copy-start.1
  17.9 0.0 copy-done
  17.9 0.2 broadcast_in_dim.30
  18.1 0.3 eq.23
  18.4 0.3 reshape.324
  18.7 0.0 copy-done.3
  18.7 0.6 broadcast.137
  19.3 0.7 reduce.9
  20.0 0.1 broadcast_in_dim.31
  20.1 0.1 copy.26
  20.2 0.1 copy.27
  20.3 2.3 %reduce-window.6 = s32[8,16,128]{2,1,0:T(8,128)S(1)} reduce-window(s32[8,16,128]{2,1,0:T(8,128)S(1)} %fusion.19, s32[]{:T(128)} %constant.11.clone.1), window={size=1x1x128 pad=0_0x0_0x127_0}, to_apply=%region_0.0 | reduce-window | flops 2080768 | bytes 131076 | tf_op jit(solution)/shard_map/reduce-window
  22.6 0.3 slice_reduce_fusion
  22.9 0.2 reduce-window.9
  23.1 0.1 add_bitcast_fusion
  23.2 0.0 copy-done.2
  23.2 0.1 and_reduce_fusion
  23.3 0.0 copy-done.1
  23.3 0.1 multiply_reduce_fusion
  23.5 8.1 %scatter_custom_fusion = s32[3072]{0:T(1024)S(1)} fusion(s32[2048]{0:T(1024)S(1)} %broadcast_select_fusion, s32[2048]{0:T(1024)S(1)} %iota.11, s32[]{:T(128)} %constant.10.clone.1), kind=kCustom, calls=%fused_computation.65 | custom fusion | bytes 12292
  31.5 0.6 gather_fusion
  32.2 1.1 %all-to-all-done = bf16[8,2,1,256,128]{4,3,1,2,0:T(8,128)(2,1)S(1)} async-done(((bf16[8,2,1,256,128]{4,3,1,2,0:T(8,128)(2,1)}), bf16[8,2,1,256,128]{4,3,1,2,0:T(8,128)(2,1)S(1)}, u32[]{:S(2)}, u32[]{:S(2)}) %all-to-all-start) | async-done | bytes 1048608 | tf_op jit(solution)/shard_map/all_to_all | solution.py:46
  33.3 0.1 copy.36
  33.4 8.7 %copy.37 = bf16[2,1,2048,128]{3,0,2,1:T(2,128)(2,1)S(1)} copy(bf16[2,1,2048,128]{3,2,0,1:T(8,128)(2,1)S(1)} %bitcast.124) | data formatting | bytes 2097152 | tf_op jit(solution)/shard_map/reshape | solution.py:45
  42.1 1.0 pad_bitcast_fusion
  43.1 10.4 %gather_fusion.1 = bf16[3072,2,128]{2,1,0:T(2,128)(2,1)S(1)} fusion(bf16[2,2049,128]{2,0,1:T(2,128)(2,1)S(1)} %pad_bitcast_fusion, s32[3072]{0:T(1024)S(1)} %broadcast_clamp_fusion), kind=kCustom, calls=%fused_computation.1 | custom fusion | bytes 3158016 | tf_op jit(solution)/shard_map/jit(_take)/gather | solution.py:23
  53.5 0.8 copy_select_fusion
  54.3 41.2 %all_to_all.23 = bf16[8,1,768,128]{3,2,1,0:T(8,128)(2,1)S(1)} all-to-all(bf16[8,1,768,128]{3,2,1,0:T(8,128)(2,1)S(1)} %bitcast.122), channel_id=1, replica_groups=mesh['chan'=8,'tm'=4] {'tm'}, dimensions={0} | all-to-all | bytes 3145728 | tf_op jit(solution)/shard_map/all_to_all | solution.py:55
  95.5 0.3 copy.56
  95.8 0.8 convolution_bitcast_fusion
  96.5 0.8 convolution_bitcast_fusion.1
  97.3 0.8 convolution_bitcast_fusion.2
  98.1 0.8 convolution_bitcast_fusion.3
  98.9 0.3 fusion.14
  99.1 0.3 fusion.12
  99.4 0.3 fusion.10
  99.7 0.3 fusion.8
  99.9 0.5 convert_add_fusion
  100.5 1.6 %copy.41 = f32[2,1,2,384,384]{4,3,2,1,0:T(8,128)} copy(f32[2,1,2,384,384]{4,3,0,2,1:T(8,128)S(1)} %convert_add_fusion) | data formatting | bytes 4718592 | tf_op jit(solution)/shard_map/add | solution.py:60
  (16 shorter events, 0.2 us)
Async XLA Ops:
  6.3 11.6 %copy-start = (s32[1024,1]{0,1:T(1,128)S(1)}, s32[1024,1]{0,1:T(1,128)}, u32[]{:S(2)}) copy-start(s32[1024,1]{0,1:T(1,128)} %param.4) | copy-start | bytes 12292
  12.6 6.1 %copy-start.3 = (s32[8]{0:T(128)S(1)}, s32[8]{0:T(128)}, u32[]{:S(2)}) copy-start(s32[8]{0:T(128)} %param.5) | copy-start | bytes 100
  12.6 20.7 %all-to-all-start = ((bf16[8,2,1,256,128]{4,3,1,2,0:T(8,128)(2,1)}), bf16[8,2,1,256,128]{4,3,1,2,0:T(8,128)(2,1)S(1)}, u32[]{:S(2)}, u32[]{:S(2)}) async-start(bf16[8,2,1,256,128]{4,3,1,2,0:T(8,128)(2,1)} %bitcast_dynamic-update-slice_fusion), calls=%async_computation | async-start | bytes 2097152 | tf_op jit(solution)/shard_map/all_to_all | solution.py:46
  17.9 5.3 %copy-start.2 = (s32[2]{0:T(128)S(1)}, s32[2]{0:T(128)}, u32[]{:S(2)}) copy-start(s32[2]{0:T(128)} %constant.36) | copy-start | bytes 28
  17.9 5.4 %copy-start.1 = (s32[2]{0:T(128)S(1)}, s32[2]{0:T(128)}, u32[]{:S(2)}) copy-start(s32[2]{0:T(128)} %constant.33) | copy-start | bytes 28
